TPU v7x, 32 devices: a whole 2x2x4 slice. The times are simulated.
32 devices in a mesh: frame: 4 (over x, core), fsdp: 4 (over z), head: 2 (over y).
Axes of the slice: x: 2, y: 2, z: 4, core: 2. Of those that a mesh axis runs over, the one named last changes fastest.
Arguments:
- queries: bfloat16 [1024, 10240], P('frame', ('fsdp', 'head')), may hold values from -6 to 6
- noisy_keys: bfloat16 [1024, 10240], P('frame', ('fsdp', 'head')), may hold values from -6 to 6
- noisy_values: bfloat16 [1024, 10240], P('frame', ('fsdp', 'head')), may hold values from -6 to 6
- clean_keys: bfloat16 [1024, 10240], P('frame', ('fsdp', 'head')), may hold values from -10 to 10
- clean_values: bfloat16 [1024, 10240], P('frame', ('fsdp', 'head')), may hold values from -6 to 6
- gain_query: float32 [5120], replicated, may hold values from 0.5 to 2
- gain_key: float32 [5120], replicated, may hold values from 0.5 to 2
- out_grad: bfloat16 [1024, 10240], P('frame', ('fsdp', 'head')), may hold values from -6 to 6
Outputs:
- attended: bfloat16 [1024, 10240], P('frame', ('fsdp', 'head'))
- grad_queries: bfloat16 [1024, 10240], P('frame', ('fsdp', 'head'))
- grad_keys: bfloat16 [1024, 10240], P('frame', ('fsdp', 'head'))
- grad_values: bfloat16 [1024, 10240], P('frame', ('fsdp', 'head'))
- grad_gain_query: float32 [5120], replicated
- grad_gain_key: float32 [5120], replicated
All inputs are finite; a program needn't handle non-finite values.
Results may differ from a plain program's by a relative error of at most 0.012.
Values may be sent and summed in bfloat16 or wider, within the bound.
A program may use at most 64 MiB of HBM per device.

v0:
```python
import math

import jax
import jax.numpy as jnp
from jax import lax
from jax.sharding import PartitionSpec as P

D = 5120
DH = 128


EPSILON = 1e-06
MASKED = -1e30


def shifted(block, axis, distance):
    devices = range(lax.axis_size(axis))
    route = [((i - distance) % len(devices), i) for i in devices]
    return lax.ppermute(block, axis, route)


def project(left_side, right_side):
    return jnp.einsum("qhd,khd->hqk", left_side, right_side, preferred_element_type=jnp.float32)


def on_device(
    queries, noisy_keys, noisy_values, clean_keys, clean_values, gain_query, gain_key, out_grad
):
    length = queries.shape[0]
    width_dev = queries.shape[1]
    head_count = width_dev // DH
    scaling = 1.0 / math.sqrt(DH)
    own_frame = lax.axis_index("frame")
    own_start = own_frame * length
    pair_reach = lax.axis_size("fsdp") // 2
    half_index = lax.axis_index("fsdp") // pair_reach
    column_start = (half_index * lax.axis_size("head") + lax.axis_index("head")) * width_dev
    gain_q = lax.dynamic_slice_in_dim(gain_query, column_start, width_dev)
    gain_k = lax.dynamic_slice_in_dim(gain_key, column_start, width_dev)

    def with_partner(stats):
        other = shifted(stats, "fsdp", pair_reach)
        return stats + other

    q_full = queries.astype(jnp.float32)
    k_full = noisy_keys.astype(jnp.float32)
    squares_q, squares_k = lax.psum(
        (jnp.sum(q_full * q_full, axis=1), jnp.sum(k_full * k_full, axis=1)), "head"
    )
    squares = with_partner(jnp.stack([squares_q, squares_k]))
    rate_q = lax.rsqrt(squares[0] / D + EPSILON)
    rate_k = lax.rsqrt(squares[1] / D + EPSILON)
    normed_q = (
        (q_full * rate_q[:, None] * gain_q).astype(jnp.bfloat16).reshape(length, head_count, DH)
    )
    normed_k = (
        (k_full * rate_k[:, None] * gain_k).astype(jnp.bfloat16).reshape(length, head_count, DH)
    )
    values_own = noisy_values.reshape(length, head_count, DH)
    grads_out = out_grad.reshape(length, head_count, DH)
    own_scores = project(normed_q, normed_k) * scaling
    row_max = jnp.max(own_scores, axis=2)
    expo = jnp.exp(own_scores - row_max[:, :, None])
    totals = jnp.sum(expo, axis=2)
    summed = jnp.einsum(
        "hqk,khd->hqd", expo.astype(jnp.bfloat16), values_own, preferred_element_type=jnp.float32
    )

    def split_piece(portion):
        key_piece, value_piece = portion
        row_count = key_piece.shape[0]
        return (
            key_piece.reshape(row_count, head_count, DH),
            value_piece.reshape(row_count, head_count, DH),
            row_count,
        )

    def visible_scores(key_piece, row_count):
        scores = project(normed_q, key_piece) * scaling
        frame_of = jnp.arange(row_count, dtype=jnp.int32) // length
        return jnp.where((frame_of < own_frame)[None, None, :], scores, MASKED)

    initial = (row_max, totals, summed)
    key_piece, value_piece, row_count = split_piece(
        (
            lax.all_gather(clean_keys, "frame", axis=0, tiled=True),
            lax.all_gather(clean_values, "frame", axis=0, tiled=True),
        )
    )

    def attend(status):
        running, denominator, accumulated = status
        scores = visible_scores(key_piece, row_count)
        newest = jnp.maximum(running, jnp.max(scores, axis=2))
        exponent = jnp.exp(scores - newest[:, :, None])
        factor = jnp.exp(running - newest)
        added = jnp.einsum(
            "hqk,khd->hqd",
            exponent.astype(jnp.bfloat16),
            value_piece,
            preferred_element_type=jnp.float32,
        )
        return (
            newest,
            denominator * factor + jnp.sum(exponent, axis=2),
            accumulated * factor[:, :, None] + added,
        )

    running, denominator, accumulated = lax.cond(
        jnp.int32(0) < own_start, attend, lambda status: status, initial
    )
    log_total = running + jnp.log(denominator)
    output_f32 = accumulated / denominator[:, :, None]
    attended = jnp.transpose(output_f32, (1, 0, 2)).reshape(length, width_dev).astype(jnp.bfloat16)
    delta = jnp.sum(jnp.transpose(grads_out.astype(jnp.float32), (1, 0, 2)) * output_f32, axis=2)
    soft_probs = jnp.exp(own_scores - log_total[:, :, None])
    grad_probs = project(grads_out, values_own)
    grad_scores = (soft_probs * (grad_probs - delta[:, :, None])).astype(jnp.bfloat16)
    grad_qn = (
        jnp.einsum("hqk,khd->qhd", grad_scores, normed_k, preferred_element_type=jnp.float32)
        * scaling
    )
    grad_kn = (
        jnp.einsum("hqk,qhd->khd", grad_scores, normed_q, preferred_element_type=jnp.float32)
        * scaling
    )
    grad_vv = jnp.einsum(
        "hqk,qhd->khd",
        soft_probs.astype(jnp.bfloat16),
        grads_out,
        preferred_element_type=jnp.float32,
    )
    reflect_key_piece, reflect_value_piece, reflect_row_count = split_piece(
        (
            lax.all_gather(clean_keys, "frame", axis=0, tiled=True),
            lax.all_gather(clean_values, "frame", axis=0, tiled=True),
        )
    )

    def attend_back(current):
        scores = visible_scores(reflect_key_piece, reflect_row_count)
        piece_probs = jnp.exp(scores - log_total[:, :, None])
        piece_grads = project(grads_out, reflect_value_piece)
        weighted = (piece_probs * (piece_grads - delta[:, :, None])).astype(jnp.bfloat16)
        return (
            current
            + jnp.einsum(
                "hqk,khd->qhd", weighted, reflect_key_piece, preferred_element_type=jnp.float32
            )
            * scaling
        )

    grad_qn = lax.cond(jnp.int32(0) < own_start, attend_back, lambda current: current, grad_qn)
    plain_q = grad_qn.reshape(length, width_dev)
    plain_k = grad_kn.reshape(length, width_dev)
    flat_q = plain_q * gain_q
    flat_k = plain_k * gain_k
    inner_q, inner_k = lax.psum(
        (jnp.sum(q_full * flat_q, axis=1), jnp.sum(k_full * flat_k, axis=1)), "head"
    )
    inners = with_partner(jnp.stack([inner_q, inner_k]))
    cube_q = rate_q * rate_q * rate_q * inners[0] / D
    cube_k = rate_k * rate_k * rate_k * inners[1] / D
    grad_queries = (rate_q[:, None] * flat_q - q_full * cube_q[:, None]).astype(jnp.bfloat16)
    grad_keys = (rate_k[:, None] * flat_k - k_full * cube_k[:, None]).astype(jnp.bfloat16)
    part_q = jnp.sum(plain_q * q_full * rate_q[:, None], axis=0)
    part_k = jnp.sum(plain_k * k_full * rate_k[:, None], axis=0)
    blank = jnp.zeros((D,), jnp.float32)
    spread_q = lax.dynamic_update_slice_in_dim(blank, part_q, column_start, 0)
    spread_k = lax.dynamic_update_slice_in_dim(blank, part_k, column_start, 0)
    grad_gain_query, grad_gain_key = lax.psum((spread_q, spread_k), ("frame", "fsdp", "head"))
    grad_values = grad_vv.reshape(length, width_dev).astype(jnp.bfloat16)
    return (attended, grad_queries, grad_keys, grad_values, grad_gain_query, grad_gain_key)


def solution(mesh):
    placed = (
        P("frame", ("fsdp", "head")),
        P("frame", ("fsdp", "head")),
        P("frame", ("fsdp", "head")),
        P("frame", ("fsdp", "head")),
        P("frame", ("fsdp", "head")),
        P(),
        P(),
        P("frame", ("fsdp", "head")),
    )
    return jax.shard_map(
        on_device,
        mesh=mesh,
        in_specs=placed,
        out_specs=(
            P("frame", ("fsdp", "head")),
            P("frame", ("fsdp", "head")),
            P("frame", ("fsdp", "head")),
            P("frame", ("fsdp", "head")),
            P(),
            P(),
        ),
        check_vma=False,
    )
```

profile of v0, /device:TPU:0, one launch (start us, length us, event | category | flops | bytes accessed | tf_op | source)
XLA Modules:
  0.0 166.8 jit_solution(3588407405975726999)
XLA Ops:
  7.2 0.7 all-gather.3.cloned.1.call-update
  8.0 2.2 %copy.46 = bf16[256,1280]{0,1:T(8,128)(2,1)} copy(bf16[256,1280]{1,0:T(8,128)(2,1)} %param.16) | data formatting | bytes 1310720 | tf_op args[4]
  11.1 5.9 %all-reduce.2 = (f32[1,256]{1,0:T(1,128)S(1)}, f32[1,256]{1,0:T(1,128)S(1)}) all-reduce(f32[1,256]{1,0:T(1,128)S(1)} %bitcast.86, f32[1,256]{1,0:T(1,128)S(1)} %bitcast.85), channel_id=1, replica_groups=mesh['frame'=4,'fsdp'=4,'head'=2] {'head'}, use_global_device_ids=true, to_apply=%region_3.4 | all-reduce | flops 512 | bytes 4096 | tf_op jit(solution)/shard_map/psum | solution.py:47
  17.0 3.2 %collective-permute-start = (f32[2,256]{1,0:T(2,128)S(1)}, f32[2,256]{1,0:T(2,128)S(1)}, u32[]{:S(2)}, u32[]{:S(2)}) collective-permute-start(f32[2,256]{1,0:T(2,128)S(1)} %pad_maximum_fusion), channel_id=1, source_target_pairs={{4,0},{6,2},{0,4},{2,6},{5,1},{7,3},{1,5},{3,7},{12,8},{14,10},{8,... | collective-permute-start | bytes 6152 | tf_op jit(solution)/shard_map/ppermute | solution.py:19
  20.2 0.8 dynamic_slice.6
  20.9 0.8 dynamic_slice.7
  21.7 1.1 copy.42
  22.8 1.1 copy.51
  24.4 0.6 multiply_reduce_fusion
  25.3 0.4 fusion.32
  25.8 1.8 %fusion.36 = f32[10,256,128]{2,1,0:T(8,128)} fusion(bf16[256,10,128]{0,2,1:T(8,128)(2,1)S(1)} %bitcast.69, f32[10,256,256]{1,2,0:T(8,128)S(1)} %get-tuple-element.167, f32[10,256]{1,0:T(8,128)S(1)} %get-tuple-element.166), kind=kOutput, calls=%fused_computation.61 | convolution fusion | flops 169738240 | bytes 4597760 | tf_op jit(solution)/shard_map/hqk,khd->hqd/dot_general | solution.py:65
  27.6 10.3 %all-gather.3.cloned.1.call-done = bf16[1024,1280]{1,0:T(8,128)(2,1)} async-done(((bf16[256,1280]{1,0:T(8,128)(2,1)}), bf16[1024,1280]{1,0:T(8,128)(2,1)}) %all-gather.3.cloned.1.call-update) | async-done | bytes 2621456 | tf_op jit(solution)/shard_map/all_gather | solution.py:86
  37.9 4.5 %copy.45 = bf16[1024,1280]{0,1:T(8,128)(2,1)} copy(bf16[1024,1280]{1,0:T(8,128)(2,1)} %all-gather.3.cloned.1.call-done) | data formatting | bytes 5242880 | tf_op jit(solution)/shard_map/all_gather | solution.py:86
  42.4 23.5 %all-gather.5.cloned.1.call-done = bf16[1024,1280]{0,1:T(8,128)(2,1)} async-done(((bf16[256,1280]{0,1:T(8,128)(2,1)}), bf16[1024,1280]{0,1:T(8,128)(2,1)}) %all-gather.5.cloned.1.call-update) | async-done | bytes 2621456 | tf_op jit(solution)/shard_map/all_gather | solution.py:87
  65.9 2.8 %copy.50 = f32[10,256,128]{1,2,0:T(8,128)} copy(f32[10,256,128]{2,1,0:T(8,128)} %get-tuple-element.144) | data formatting | bytes 2621440 | tf_op jit(solution)/shard_map/cond | solution.py:109
  68.7 2.7 %convolution_convert_fusion = bf16[10,256,128]{1,2,0:T(8,128)(2,1)} fusion(bf16[256,10,128]{0,2,1:T(8,128)(2,1)} %bitcast.65, f32[10,256,256]{1,2,0:T(8,128)S(1)} %get-tuple-element.167, f32[10,256]{1,0:T(8,128)S(1)} %log_add_fusion), kind=kOutput, calls=%fused_computation.60 | convolution fusion | flops 170065920 | bytes 3942400 | tf_op jit(solution)/shard_map/hqk,qhd->khd/dot_general | solution.py:127
  71.5 1.1 fusion.54
  72.5 0.8 multiply_convert_fusion.8
  73.6 1.4 fusion.34
  75.0 0.6 convolution_multiply_fusion
  75.6 0.7 fusion.53
  76.3 0.9 copy-done
  77.3 2.1 %fusion.45 = (f32[1280]{0:T(1024)S(1)}, f32[256]{0:T(256)S(1)}) fusion(f32[256,1280]{0,1:T(8,128)} %get-tuple-element.92, bf16[256,1280]{0,1:T(8,128)(2,1)S(1)} %copy.38, f32[256]{0:T(256)S(1)} %bitcast.76, f32[1280]{0:T(1024)S(1)} %dynamic_slice.6), kind=kLoop, calls=%fused_computation.69 | loop fusion | flops 2292224 | bytes 1978368 | tf_op jit(solution)/shard_map/reduce_sum | solution.py:166
  79.4 4.9 %all-reduce.1 = (f32[1,256]{1,0:T(1,128)S(1)}, f32[1,256]{1,0:T(1,128)S(1)}) all-reduce(f32[1,256]{1,0:T(1,128)S(1)} %bitcast.83, f32[1,256]{1,0:T(1,128)S(1)} %bitcast.84), channel_id=1, replica_groups=mesh['frame'=4,'fsdp'=4,'head'=2] {'head'}, use_global_device_ids=true, to_apply=%region_16.17 | all-reduce | flops 512 | bytes 4096 | tf_op jit(solution)/shard_map/psum | solution.py:158
  84.3 2.5 %collective-permute-start.1 = (f32[2,256]{1,0:T(2,128)S(1)}, f32[2,256]{1,0:T(2,128)S(1)}, u32[]{:S(2)}, u32[]{:S(2)}) collective-permute-start(f32[2,256]{1,0:T(2,128)S(1)} %pad_maximum_fusion.1), channel_id=1, source_target_pairs={{4,0},{6,2},{0,4},{2,6},{5,1},{7,3},{1,5},{3,7},{12,8},{14,10},{8,... | collective-permute-start | bytes 6152 | tf_op jit(solution)/shard_map/ppermute | solution.py:19
  87.0 0.3 dynamic_update_slice.6
  87.3 65.2 %all-reduce = (f32[5120]{0:T(1024)}, f32[5120]{0:T(1024)}) all-reduce(f32[5120]{0:T(1024)S(1)} %dynamic_update_slice.6, f32[5120]{0:T(1024)S(1)} %dynamic_update_slice.7), channel_id=1, replica_groups=mesh['frame'=4,'fsdp'=4,'head'=2] {'frame','fsdp','head'}, use_global_device_ids=true, to_apply=%region_18.19 | all-reduce | flops 10240 | bytes 81920 | tf_op jit(solution)/shard_map/psum | solution.py:171
  152.6 2.2 %copy.64 = bf16[256,1280]{1,0:T(8,128)(2,1)} copy(bf16[256,1280]{0,1:T(8,128)(2,1)} %bitcast.74) | data formatting | bytes 1310720
  154.8 1.1 copy.61
  156.2 1.1 copy.63
  157.3 1.6 fusion.43
  158.9 1.1 copy.62
  (63 shorter events, 2.7 us)
Async XLA Ops:
  7.2 3.0 %copy-start.17 = (bf16[256,1280]{1,0:T(8,128)(2,1)S(1)}, bf16[256,1280]{1,0:T(8,128)(2,1)}, u32[]{:S(2)}) copy-start(bf16[256,1280]{1,0:T(8,128)(2,1)} %param.12) | copy-start | bytes 1966084
  7.2 3.2 %copy-start.18 = (bf16[256,1280]{1,0:T(8,128)(2,1)S(1)}, bf16[256,1280]{1,0:T(8,128)(2,1)}, u32[]{:S(2)}) copy-start(bf16[256,1280]{1,0:T(8,128)(2,1)} %param.13) | copy-start | bytes 1966084
  7.2 30.7 %all-gather.3.cloned.1.call-start = ((), (), s32[]{:S(2)}) async-start(), calls=%async_computation | async-start | bytes 3276800 | tf_op jit(solution)/shard_map/all_gather | solution.py:86
  7.9 58.0 %all-gather.5.cloned.1.call-start = ((), (), s32[]{:S(2)}) async-start(), calls=%async_computation.1 | async-start | bytes 3276800 | tf_op jit(solution)/shard_map/all_gather | solution.py:87
  10.1 11.6 %copy-start.19 = (bf16[256,1280]{1,0:T(8,128)(2,1)S(1)}, bf16[256,1280]{1,0:T(8,128)(2,1)}, u32[]{:S(2)}) copy-start(bf16[256,1280]{1,0:T(8,128)(2,1)} %param.14) | copy-start | bytes 1966084
  10.2 12.6 %copy-start.20 = (bf16[256,1280]{1,0:T(8,128)(2,1)S(1)}, bf16[256,1280]{1,0:T(8,128)(2,1)}, u32[]{:S(2)}) copy-start(bf16[256,1280]{1,0:T(8,128)(2,1)} %param.19) | copy-start | bytes 1966084
  10.7 13.5 %copy-start.1 = (bf16[256,1280]{0,1:T(8,128)(2,1)}, bf16[256,1280]{0,1:T(8,128)(2,1)S(1)}, u32[]{:S(2)}) copy-start(bf16[256,1280]{0,1:T(8,128)(2,1)S(1)} %copy.39) | copy-start | bytes 1966084
  17.0 6.9 %collective-permute-start = (f32[2,256]{1,0:T(2,128)S(1)}, f32[2,256]{1,0:T(2,128)S(1)}, u32[]{:S(2)}, u32[]{:S(2)}) collective-permute-start(f32[2,256]{1,0:T(2,128)S(1)} %pad_maximum_fusion), channel_id=1, source_target_pairs={{4,0},{6,2},{0,4},{2,6},{5,1},{7,3},{1,5},{3,7},{12,8},{14,10},{8,... | collective-permute-start | bytes 6152 | tf_op jit(solution)/shard_map/ppermute | solution.py:19
  24.2 0.9 copy-start.4
  24.4 0.9 copy-start.11
  24.4 1.4 copy-start.9
  68.7 2.8 %copy-start.8 = (bf16[256,1280]{0,1:T(8,128)(2,1)S(1)}, bf16[256,1280]{0,1:T(8,128)(2,1)}, u32[]{:S(2)}) copy-start(bf16[256,1280]{0,1:T(8,128)(2,1)} %copy.51) | copy-start | bytes 1966084
  68.7 2.8 %copy-start.13 = (f32[10,256,128]{1,2,0:T(8,128)S(1)}, f32[10,256,128]{1,2,0:T(8,128)}, u32[]{:S(2)}) copy-start(f32[10,256,128]{1,2,0:T(8,128)} %copy.50) | copy-start | bytes 3932164
  68.7 3.8 %copy-start.10 = (bf16[256,1280]{0,1:T(8,128)(2,1)S(1)}, bf16[256,1280]{0,1:T(8,128)(2,1)}, u32[]{:S(2)}) copy-start(bf16[256,1280]{0,1:T(8,128)(2,1)} %copy.42) | copy-start | bytes 1966084
  72.5 1.1 copy-start.12
  73.6 1.4 copy-start.5
  73.6 2.0 %copy-start.2 = (bf16[256,1280]{0,1:T(8,128)(2,1)S(1)}, bf16[256,1280]{0,1:T(8,128)(2,1)}, u32[]{:S(2)}) copy-start(bf16[256,1280]{0,1:T(8,128)(2,1)} %copy-done.1) | copy-start | bytes 1966084
  75.0 2.2 %copy-start = (bf16[1024,1280]{0,1:T(8,128)(2,1)S(1)}, bf16[1024,1280]{0,1:T(8,128)(2,1)}, u32[]{:S(2)}) copy-start(bf16[1024,1280]{0,1:T(8,128)(2,1)} %copy.45) | copy-start | bytes 7864324
  75.6 1.6 copy-start.6
  77.3 77.5 %copy-start.16 = (bf16[10,256,128]{1,2,0:T(8,128)(2,1)S(1)}, bf16[10,256,128]{1,2,0:T(8,128)(2,1)}, u32[]{:S(2)}) copy-start(bf16[10,256,128]{1,2,0:T(8,128)(2,1)} %get-tuple-element.161) | copy-start | bytes 1966084
  77.3 78.6 %copy-start.3 = (bf16[256,1280]{0,1:T(8,128)(2,1)S(1)}, bf16[256,1280]{0,1:T(8,128)(2,1)}, u32[]{:S(2)}) copy-start(bf16[256,1280]{0,1:T(8,128)(2,1)} %copy-done.1) | copy-start | bytes 1966084
  77.3 78.6 %copy-start.7 = (f32[10,128,256]{2,1,0:T(8,128)S(1)}, f32[10,128,256]{2,1,0:T(8,128)}, u32[]{:S(2)}) copy-start(f32[10,128,256]{2,1,0:T(8,128)} %copy-done.6) | copy-start | bytes 3932164
  84.3 71.5 %collective-permute-start.1 = (f32[2,256]{1,0:T(2,128)S(1)}, f32[2,256]{1,0:T(2,128)S(1)}, u32[]{:S(2)}, u32[]{:S(2)}) collective-permute-start(f32[2,256]{1,0:T(2,128)S(1)} %pad_maximum_fusion.1), channel_id=1, source_target_pairs={{4,0},{6,2},{0,4},{2,6},{5,1},{7,3},{1,5},{3,7},{12,8},{14,10},{8,... | collective-permute-start | bytes 6152 | tf_op jit(solution)/shard_map/ppermute | solution.py:19
Sparse Core Ops, SparseCore 0:
  9.6 28.2 all-gather.2
  40.0 25.8 all-gather.4
where the time goes:
time: 167 us
  blocking collectives  76.1 us (46%)
  waiting for transfers between devices  34.5 us (21%)
  local copies, waits for them, and re-layouts  21.2 us (13%)
  between operations  14.3 us (9%)
  matrix products  7.9 us (5%)
  other arithmetic  7.13 us (4%)
  starting transfers between devices  5.7 us (3%)
    psum x1, blocking collectives, on_device(): lax.psum((spread_q, spread_k), ('frame', 'fsdp', 'head'))  65.2 us
    all_gather x1, waiting for transfers between devices, on_device(): lax.all_gather(clean_values, 'frame', axis=0, tiled=True)  23.5 us
    unnamed x47, local copies, waits for them, and re-layouts  11.8 us
    all_gather x1, waiting for transfers between devices, on_device(): lax.all_gather(clean_keys, 'frame', axis=0, tiled=True)  10.3 us
    psum x1, blocking collectives, on_device(): lax.psum((jnp.sum(q_full * q_full, axis=1), jnp.sum(k_full * k_full, axis...  5.89 us
    ppermute x2, starting transfers between devices, shifted(): return lax.ppermute(block, axis, route)  5.62 us
    psum x1, blocking collectives, on_device(): lax.psum((jnp.sum(q_full * flat_q, axis=1), jnp.sum(k_full * flat_k, axis...  4.93 us
    all_gather x1, local copies, waits for them, and re-layouts, on_device(): lax.all_gather(clean_keys, 'frame', axis=0, tiled=True)  4.54 us
  transfers between devices with their start and end apart: 4, of which 2 were waited for; matrix products, arithmetic and copies ran while one was open for 11% of the time, Pallas kernels for 0%

commit v1 on v0

v1 whole, which is shorter than its diff:
```python
import functools
import math

import jax
import jax.numpy as jnp
from jax import lax
from jax.experimental import pallas as pl
from jax.experimental.pallas import tpu as pltpu
from jax.sharding import PartitionSpec as P

DH = 128
EPSILON = 1e-06
MESH = pl.DeviceIdType.MESH
F32 = jnp.float32
BF16 = jnp.bfloat16


def dot_nt(a, b):
    return lax.dot_general(a, b, (((1,), (1,)), ((), ())), preferred_element_type=F32)


def dot_nn(a, b):
    return lax.dot_general(a, b, (((1,), (0,)), ((), ())), preferred_element_type=F32)


def dot_tn(a, b):
    return lax.dot_general(a, b, (((0,), (0,)), ((), ())), preferred_element_type=F32)


def kernel(
    frames, fsdp, heads_axis, width, features,
    q_hbm, k_hbm, v_hbm, ck_hbm, cv_hbm, gq_hbm, gk_hbm, g_hbm,
    att_out, dq_out, dk_out, dv_out, gain_q_out, gain_k_out,
    q, k, v, g, gq, gk, cks, cvs, flat_q, flat_k, inner_q, inner_k, rates,
    stats, sums1, sums2,
    load_sem, own_send, relay_send, clean_recv, stats_send, stats_recv, s1_send, s1_recv, s2_send, s2_recv,
):
    length = q.shape[0]
    head_count = width // DH
    videos = fsdp // 2
    scaling = 1.0 / math.sqrt(DH)
    power = scaling * math.log2(math.e)
    frame = lax.axis_index("frame")
    fs = lax.axis_index("fsdp")
    half = fs // videos
    video = lax.rem(fs, videos)
    me1 = frame * videos + video
    n1 = frames * videos
    me2 = half * heads_axis + lax.axis_index("head")
    n2 = 2 * heads_axis

    def peer1(distance):
        p = lax.rem(me1 + distance, n1)
        return {"frame": p // videos, "fsdp": half * videos + lax.rem(p, videos)}

    def peer2(distance):
        p = lax.rem(me2 + distance, n2)
        return {"fsdp": (p // heads_axis) * videos + video, "head": lax.rem(p, heads_axis)}

    barrier = pltpu.get_barrier_semaphore()

    def greet(d, _):
        pl.semaphore_signal(barrier, inc=1, device_id=peer1(d), device_id_type=MESH)
        return 0

    lax.fori_loop(1, n1, greet, 0)
    for d in range(1, n2):
        pl.semaphore_signal(barrier, inc=1, device_id=peer2(d), device_id_type=MESH)
    start = pl.multiple_of(me2 * width, DH)
    loads = []
    for i, (src, dst) in enumerate(
        (
            (q_hbm, q),
            (k_hbm, k),
            (gq_hbm.at[:, pl.ds(start, width)], gq),
            (gk_hbm.at[:, pl.ds(start, width)], gk),
            (v_hbm, v),
            (g_hbm, g),
        )
    ):
        copy = pltpu.make_async_copy(src, dst, load_sem.at[i])
        copy.start()
        loads.append(copy)
    pl.semaphore_wait(barrier, n1 - 1 + n2 - 1)

    def columns(h):
        return pl.ds(pl.multiple_of(h * DH, DH), DH)

    def clean_copy(j, h, kv, target, sends, own):
        cols = columns(h)
        land = (cks, cvs)[kv].at[j, :, cols]
        src = (ck_hbm, cv_hbm)[kv].at[:, cols] if own else land
        return pltpu.make_async_remote_copy(
            src_ref=src,
            dst_ref=land,
            send_sem=sends.at[h, kv],
            recv_sem=clean_recv.at[j, h, kv],
            device_id={"frame": jnp.int32(target)},
            device_id_type=MESH,
        )

    def plan(nb):
        pair, side = nb // 2, nb % 2
        partner, further = 2 * pair + 1 - side, nb + 2
        direct = [2 * c + side for c in range(pair)]
        relayed = [2 * c + 1 - side for c in range(pair)] + ([nb - 1] if side else [])
        own = ([further] if further < frames else []) + ([partner] if side == 0 else [])
        passes = [partner] + ([further] if further < frames else [])
        return direct, relayed, own, passes

    for nb in range(frames):
        _, _, own, _ = plan(nb)
        if own:

            @pl.when(frame == nb)
            def _():
                def go(h, _):
                    for t, target in enumerate(own):
                        for kv in range(2):
                            clean_copy(nb, h, kv, target, own_send.at[t], True).start()
                    return 0

                lax.fori_loop(0, head_count, go, 0)

    row = lax.broadcasted_iota(jnp.int32, (8, length), 0)

    def as_rows(a, b):
        a = jnp.sum(jnp.transpose(a), axis=0, keepdims=True)
        b = jnp.sum(jnp.transpose(b), axis=0, keepdims=True)
        return jnp.where(row == 0, a, jnp.where(row == 1, b, 0.0))

    def stats_copy(phase, d, slot):
        return pltpu.make_async_remote_copy(
            src_ref=stats.at[phase, slot],
            dst_ref=stats.at[phase, slot],
            send_sem=stats_send.at[phase, d],
            recv_sem=stats_recv.at[phase, d],
            device_id=peer2(d),
            device_id_type=MESH,
        )

    def stats_go(phase, value):
        stats[phase, me2] = value
        for d in range(1, n2):
            stats_copy(phase, d, me2).start()

    def stats_total(phase):
        for d in range(1, n2):
            stats_copy(phase, d, lax.rem(me2 + n2 - d, n2)).wait_recv()
        return jnp.sum(stats[phase], axis=0)

    loads[0].wait()
    loads[1].wait()

    def square(ref):
        total = jnp.zeros((length, DH), F32)
        for h in range(head_count):
            x = ref[:, h * DH : (h + 1) * DH].astype(F32)
            total = total + x * x
        return total

    stats_go(0, as_rows(square(q), square(k)))
    inner_q[...] = jnp.zeros_like(inner_q)
    inner_k[...] = jnp.zeros_like(inner_k)
    for copy in loads[2:]:
        copy.wait()
    rates[...] = jnp.transpose(lax.rsqrt(stats_total(0) / features + EPSILON))

    def head_step(nb, h):
        direct, relayed, _, passes = plan(nb)
        cols = columns(h)
        for j in direct:
            for kv in range(2):
                clean_copy(j, h, kv, passes[0], relay_send.at[0, j], False).wait_recv()
                for t, target in enumerate(passes):
                    clean_copy(j, h, kv, target, relay_send.at[t, j], False).start()
        rate_q = rates[:, 0:1]
        rate_k = rates[:, 1:2]
        q_full = q[:, cols].astype(F32)
        k_full = k[:, cols].astype(F32)
        gain_q = gq[:, cols]
        gain_k = gk[:, cols]
        qn = (q_full * rate_q * gain_q).astype(BF16)
        kn = (k_full * rate_k * gain_k).astype(BF16)
        val = v[:, cols]
        grad = g[:, cols]
        scores = [dot_nt(qn, kn)]
        grad_probs = [dot_nt(grad, val)]
        for j in relayed:
            for kv in range(2):
                clean_copy(j, h, kv, passes[0], relay_send.at[0, j], False).wait_recv()
        for j in range(nb):
            scores.append(dot_nt(qn, cks[j, :, cols]))
            grad_probs.append(dot_nt(grad, cvs[j, :, cols]))
        top = functools.reduce(jnp.maximum, [jnp.max(s, axis=1, keepdims=True) for s in scores])
        expo = [jnp.exp2((s - top) * power) for s in scores]
        total = functools.reduce(jnp.add, [jnp.sum(e, axis=1, keepdims=True) for e in expo])
        summed = dot_nn(expo[0].astype(BF16), val)
        for j in range(nb):
            summed = summed + dot_nn(expo[j + 1].astype(BF16), cvs[j, :, cols])
        inverse = 1.0 / total
        attention = summed * inverse
        att_out[:, cols] = attention.astype(BF16)
        delta = jnp.sum(grad.astype(F32) * attention, axis=1, keepdims=True)
        probs = [e * inverse for e in expo]
        grad_scores = [(p * (d - delta)).astype(BF16) for p, d in zip(probs, grad_probs)]
        grad_qn = dot_nn(grad_scores[0], kn)
        for j in range(nb):
            grad_qn = grad_qn + dot_nn(grad_scores[j + 1], cks[j, :, cols])
        grad_qn = grad_qn * scaling
        grad_kn = dot_tn(grad_scores[0], qn) * scaling
        dv_out[:, cols] = dot_tn(probs[0].astype(BF16), grad).astype(BF16)
        fq = grad_qn * gain_q
        fk = grad_kn * gain_k
        flat_q[:, cols] = fq
        flat_k[:, cols] = fk
        inner_q[...] += q_full * fq
        inner_k[...] += k_full * fk
        sums1[me1, 0:1, cols] = jnp.sum(grad_qn * q_full * rate_q, axis=0, keepdims=True)
        sums1[me1, 1:2, cols] = jnp.sum(grad_kn * k_full * rate_k, axis=0, keepdims=True)

    for nb in range(frames):

        @pl.when(frame == nb)
        def _():
            def step(h, _):
                head_step(nb, h)
                return 0

            lax.fori_loop(0, head_count, step, 0)

    stats_go(1, as_rows(inner_q[...], inner_k[...]))

    def s1_copy(d, slot):
        return pltpu.make_async_remote_copy(
            src_ref=sums1.at[slot],
            dst_ref=sums1.at[slot],
            send_sem=s1_send.at[d],
            recv_sem=s1_recv.at[d],
            device_id=peer1(d),
            device_id_type=MESH,
        )

    def s2_copy(d, slot):
        return pltpu.make_async_remote_copy(
            src_ref=sums2.at[slot],
            dst_ref=sums2.at[slot],
            send_sem=s2_send.at[d],
            recv_sem=s2_recv.at[d],
            device_id=peer2(d),
            device_id_type=MESH,
        )

    def s1_go(d, _):
        s1_copy(d, me1).start()
        return 0

    lax.fori_loop(1, n1, s1_go, 0)

    inners = jnp.transpose(stats_total(1))
    rate_q = rates[:, 0:1]
    rate_k = rates[:, 1:2]
    cube_q = rate_q * rate_q * rate_q * inners[:, 0:1] / features
    cube_k = rate_k * rate_k * rate_k * inners[:, 1:2] / features

    def s1_land(d, _):
        s1_copy(d, lax.rem(me1 + n1 - d, n1)).wait_recv()
        return 0

    lax.fori_loop(1, n1, s1_land, 0)
    sums2[me2] = jnp.sum(sums1[...], axis=0)
    for d in range(1, n2):
        s2_copy(d, me2).start()

    def finish(h, _):
        cols = columns(h)
        dq_out[:, cols] = (rate_q * flat_q[:, cols] - q[:, cols].astype(F32) * cube_q).astype(BF16)
        dk_out[:, cols] = (rate_k * flat_k[:, cols] - k[:, cols].astype(F32) * cube_k).astype(BF16)
        return 0

    lax.fori_loop(0, head_count, finish, 0)
    for d in range(1, n2):
        s2_copy(d, lax.rem(me2 + n2 - d, n2)).wait_recv()
    for p in range(n2):
        gain_q_out[:, p * width : (p + 1) * width] = sums2[p, 0:1, :]
        gain_k_out[:, p * width : (p + 1) * width] = sums2[p, 1:2, :]

    for d in range(1, n2):
        stats_copy(0, d, me2).wait_send()
        stats_copy(1, d, me2).wait_send()
        s2_copy(d, me2).wait_send()

    def s1_gone(d, _):
        s1_copy(d, me1).wait_send()
        return 0

    lax.fori_loop(1, n1, s1_gone, 0)
    for nb in range(frames):
        direct, _, own, passes = plan(nb)

        @pl.when(frame == nb)
        def _():
            def gone(h, _):
                for kv in range(2):
                    for t, target in enumerate(own):
                        clean_copy(nb, h, kv, target, own_send.at[t], True).wait_send()
                    for j in direct:
                        for t, target in enumerate(passes):
                            clean_copy(j, h, kv, target, relay_send.at[t, j], False).wait_send()
                return 0

            lax.fori_loop(0, head_count, gone, 0)


def on_device(queries, noisy_keys, noisy_values, clean_keys, clean_values, gain_query, gain_key, out_grad):
    length, width = queries.shape
    features = gain_query.shape[0]
    frames = lax.axis_size("frame")
    fsdp = lax.axis_size("fsdp")
    heads_axis = lax.axis_size("head")
    head_count = width // DH
    n1 = frames * (fsdp // 2)
    n2 = 2 * heads_axis
    block = jax.ShapeDtypeStruct((length, width), BF16)
    gains = jax.ShapeDtypeStruct((1, features), F32)
    anywhere = pl.BlockSpec(memory_space=pl.ANY)
    vmem = pl.BlockSpec(memory_space=pltpu.VMEM)
    dma = pltpu.SemaphoreType.DMA
    earlier = max(frames - 1, 1)
    outs = pl.pallas_call(
        functools.partial(kernel, frames, fsdp, heads_axis, width, features),
        out_shape=(block, block, block, block, gains, gains),
        in_specs=[anywhere] * 8,
        out_specs=[vmem] * 6,
        scratch_shapes=[
            pltpu.VMEM((length, width), BF16),
            pltpu.VMEM((length, width), BF16),
            pltpu.VMEM((length, width), BF16),
            pltpu.VMEM((length, width), BF16),
            pltpu.VMEM((1, width), F32),
            pltpu.VMEM((1, width), F32),
            pltpu.VMEM((earlier, length, width), BF16),
            pltpu.VMEM((earlier, length, width), BF16),
            pltpu.VMEM((length, width), F32),
            pltpu.VMEM((length, width), F32),
            pltpu.VMEM((length, DH), F32),
            pltpu.VMEM((length, DH), F32),
            pltpu.VMEM((length, 8), F32),
            pltpu.VMEM((2, n2, 8, length), F32),
            pltpu.VMEM((n1, 2, width), F32),
            pltpu.VMEM((n2, 2, width), F32),
            dma((6,)),
            dma((2, head_count, 2)),
            dma((2, earlier, head_count, 2)),
            dma((earlier, head_count, 2)),
            dma((2, n2)),
            dma((2, n2)),
            dma((n1,)),
            dma((n1,)),
            dma((n2,)),
            dma((n2,)),
        ],
        compiler_params=pltpu.CompilerParams(collective_id=0, has_side_effects=True),
        name="attention",
    )(
        queries, noisy_keys, noisy_values, clean_keys, clean_values,
        gain_query.reshape(1, features), gain_key.reshape(1, features), out_grad,
    )
    return (*outs[:4], outs[4].reshape(features), outs[5].reshape(features))


def solution(mesh):
    tokens = P("frame", ("fsdp", "head"))
    return jax.shard_map(
        on_device,
        mesh=mesh,
        in_specs=(tokens, tokens, tokens, tokens, tokens, P(), P(), tokens),
        out_specs=(tokens, tokens, tokens, tokens, P(), P()),
        check_vma=False,
    )
```

time: 167 us -> 57.5 us (0.34)
  blocking collectives: 76.1 us -> 0 us
  Pallas kernels: 0 us -> 49.6 us
  waiting for transfers between devices: 34.5 us -> 0 us
  local copies, waits for them, and re-layouts: 21.2 us -> 6.86 us
  between operations: 14.3 us -> 0.66 us
  matrix products: 7.9 us -> 0 us
  other arithmetic: 7.13 us -> 0 us
  starting transfers between devices: 5.7 us -> 0 us
    psum x3 -> x0, blocking collectives: 76.1 us -> none  [the longest x1 65.2 us: on_device(): lax.psum((spread_q, spread_k), ('frame', 'fsdp', 'head'))]
    pallas_call x0 -> x1, Pallas kernels: none -> 49.6 us  [on_device(): pl.pallas_call(functools.partial(kernel, frames, fsdp, heads_axis, width,...]
    all_gather x2 -> x0, waiting for transfers between devices: 33.8 us -> none  [the longest x1 23.5 us: on_device(): lax.all_gather(clean_values, 'frame', axis=0, tiled=True)]
    dot_general x6 -> x0, matrix products: 7.9 us -> none  [the longest x1 2.73 us: on_device(): jnp.einsum('hqk,qhd->khd', soft_probs.astype(jnp.bfloat16), grads_out, pr...]
    ppermute x2 -> x0, starting transfers between devices: 5.62 us -> none  [shifted(): return lax.ppermute(block, axis, route)]
    unnamed x47 -> x16, local copies, waits for them, and re-layouts: 11.8 us -> 6.86 us
    reduce_sum x6 -> x0, other arithmetic: 4.72 us -> none  [the longest x1 2.12 us: on_device(): part_q = jnp.sum(plain_q * q_full * rate_q[:, None], axis=0)]
    all_gather x1 -> x0, local copies, waits for them, and re-layouts: 4.54 us -> none  [on_device(): lax.all_gather(clean_keys, 'frame', axis=0, tiled=True)]
  transfers between devices with their start and end apart: 4 -> 0, of which waited for: 2 -> 0; matrix products, arithmetic and copies ran while one was open for 11% -> 0% of each run, Pallas kernels for 0% -> 0%
where the time goes in v1:
time: 57.5 us; the launch traced here: 57.2 us
  Pallas kernels  49.6 us (86%)
  local copies, waits for them, and re-layouts  6.86 us (12%)
  between operations  0.66 us (1%)
    pallas_call x1, Pallas kernels, on_device(): pl.pallas_call(functools.partial(kernel, frames, fsdp, heads_axis, width,...  49.6 us
    unnamed x16, local copies, waits for them, and re-layouts  6.86 us

profile of v1, /device:TPU:0, one launch (start us, length us, event | category | flops | bytes accessed | tf_op | source)
XLA Modules:
  0.0 57.2 jit_solution(3946384299260683252)
XLA Ops:
  0.6 49.6 %attention.1 = (bf16[256,1280]{1,0:T(8,128)(2,1)}, bf16[256,1280]{1,0:T(8,128)(2,1)}, bf16[256,1280]{1,0:T(8,128)(2,1)}, bf16[256,1280]{1,0:T(8,128)(2,1)}, f32[1,5120]{1,0:T(1,128)}, /*index=5*/f32[1,5120]{1,0:T(1,128)}) custom-call(bf16[256,1280]{1,0:T(8,128)(2,1)} %q_hbm.1, bf16[256,1280]{1,0:T(8,128)(2,1)} %k_hbm.1, bf16[256,1280]{1,0:T(8,128)(2,1)} %v_hbm.1, ...), custom_call_target="tpu_custom_call" | custom-call | tf_op jit(solution)/shard_map/attention/pallas_call | solution.py:330
  50.3 0.0 copy-start.2
  50.3 2.0 %copy.20 = bf16[256,1280]{1,0:T(8,128)(2,1)} copy(bf16[256,1280]{1,0:T(8,128)(2,1)} %get-tuple-element.24) | data formatting | bytes 1310720
  52.3 0.0 copy-done.2
  52.3 0.0 copy-start.1
  52.3 0.8 %copy.21 = bf16[256,1280]{1,0:T(8,128)(2,1)} copy(bf16[256,1280]{1,0:T(8,128)(2,1)S(1)} %copy-done.2) | data formatting | bytes 1310720
  53.2 0.5 copy-done.1
  53.6 0.0 copy-start
  53.6 0.8 %copy.22 = bf16[256,1280]{1,0:T(8,128)(2,1)} copy(bf16[256,1280]{1,0:T(8,128)(2,1)S(1)} %copy-done.1) | data formatting | bytes 1310720
  54.5 0.5 copy-done
  55.0 0.0 copy-start.4
  55.0 0.8 %copy.23 = bf16[256,1280]{1,0:T(8,128)(2,1)} copy(bf16[256,1280]{1,0:T(8,128)(2,1)S(1)} %copy-done) | data formatting | bytes 1310720
  55.8 0.0 copy-done.4
  55.8 0.0 copy-start.3
  55.8 0.6 %copy.24 = f32[5120]{0:T(1024)} copy(f32[5120]{0:T(1024)S(1)} %bitcast.5) | data formatting | bytes 40960
  56.4 0.1 copy-done.3
  56.5 0.6 %copy.25 = f32[5120]{0:T(1024)} copy(f32[5120]{0:T(1024)S(1)} %bitcast.4) | data formatting | bytes 40960
Async XLA Ops:
  50.3 2.0 %copy-start.2 = (bf16[256,1280]{1,0:T(8,128)(2,1)S(1)}, bf16[256,1280]{1,0:T(8,128)(2,1)}, u32[]{:S(2)}) copy-start(bf16[256,1280]{1,0:T(8,128)(2,1)} %get-tuple-element.25) | copy-start | bytes 1966084
  52.3 1.3 %copy-start.1 = (bf16[256,1280]{1,0:T(8,128)(2,1)S(1)}, bf16[256,1280]{1,0:T(8,128)(2,1)}, u32[]{:S(2)}) copy-start(bf16[256,1280]{1,0:T(8,128)(2,1)} %get-tuple-element.26) | copy-start | bytes 1966084
  53.6 1.3 %copy-start = (bf16[256,1280]{1,0:T(8,128)(2,1)S(1)}, bf16[256,1280]{1,0:T(8,128)(2,1)}, u32[]{:S(2)}) copy-start(bf16[256,1280]{1,0:T(8,128)(2,1)} %get-tuple-element.27) | copy-start | bytes 1966084
  55.0 0.8 %copy-start.4 = (f32[1,5120]{1,0:T(1,128)S(1)}, f32[1,5120]{1,0:T(1,128)}, u32[]{:S(2)}) copy-start(f32[1,5120]{1,0:T(1,128)} %get-tuple-element.16) | copy-start | bytes 61444
  55.8 0.7 %copy-start.3 = (f32[1,5120]{1,0:T(1,128)S(1)}, f32[1,5120]{1,0:T(1,128)}, u32[]{:S(2)}) copy-start(f32[1,5120]{1,0:T(1,128)} %get-tuple-element.17) | copy-start | bytes 61444
